TPU v7x, 32 devices: a whole 2x2x4 slice. The times are simulated.
32 devices in a mesh: ep: 8 (over z, y), dp: 4 (over x, core).
Axes of the slice: x: 2, y: 2, z: 4, core: 2. Of those that a mesh axis runs over, the one named last changes fastest.
Arguments:
- activations: float32 [16, 256, 768], P('ep', 'dp'), may hold values from -6 to 6
- out_grads: float32 [16, 256, 512], P('ep', 'dp'), may hold values from -6 to 6
- counts: int32 [16, 4], P('ep', 'dp'), may hold values from 1 to 64
- slot_weights: float32 [16, 768, 512], P('ep', None, 'dp'), may hold values from -0.21875 to 0.21875
- master: float32 [8, 768, 512], P(None, 'ep', 'dp'), may hold values from -0.21875 to 0.21875
- moment_one: float32 [8, 768, 512], P(None, 'ep', 'dp'), may hold values from -6 to 6
- moment_two: float32 [8, 768, 512], P(None, 'ep', 'dp'), may hold values from 1 to 100
- old_table: int32 [16, 1], replicated, may hold values from 0 to 7
- new_table: int32 [16, 1], replicated, may hold values from 0 to 7
Outputs:
- outputs: float32 [16, 256, 512], P('ep', 'dp')
- input_grads: float32 [16, 256, 768], P('ep', 'dp')
- new_master: float32 [8, 768, 512], P(None, 'ep', 'dp')
- new_moment_one: float32 [8, 768, 512], P(None, 'ep', 'dp')
- new_moment_two: float32 [8, 768, 512], P(None, 'ep', 'dp')
- new_slots: float32 [16, 768, 512], P('ep', None, 'dp')
Inputs may be any that keep to these rules, and one draw needn't show every extreme that they name: `old_table`: every expert is named by at least one old slot. `new_table`: every expert is named by at least one new slot.
All inputs are finite; a program needn't handle non-finite values.
Results may differ from a plain program's by a relative error of at most 0.00007.
Values sent between devices are 32-bit elements; how exact they have to be, the bound alone decides.
A program may use at most 64 MiB of HBM per device.

v0:
```python
import functools

import jax
import jax.numpy as jnp
from jax import lax
from jax.experimental import pallas as pl
from jax.experimental.pallas import tpu as pltpu
from jax.sharding import PartitionSpec as P

STEP = 100
beta_one = 0.9
beta_two = 0.999
learn_rate = 0.02
epsilon = 1e-08
decay_rate = 0.1

MESH = pl.DeviceIdType.MESH


def adamw(master, moment_one, moment_two, expert_grad):
    first_new = beta_one * moment_one + (1.0 - beta_one) * expert_grad
    second_new = beta_two * moment_two + (1.0 - beta_two) * expert_grad * expert_grad
    first_hat = first_new / (1.0 - beta_one**STEP)
    second_hat = second_new / (1.0 - beta_two**STEP)
    updated = master - learn_rate * (
        first_hat / (jnp.sqrt(second_hat) + epsilon) + decay_rate * master
    )
    return (updated, first_new, second_new)


def split(x):
    high = x.astype(jnp.bfloat16)
    low = (x - high.astype(jnp.float32)).astype(jnp.bfloat16)
    return high, low


def dot3(a, b, dims):
    def one(p, q):
        return lax.dot_general(p, q, (dims, ((), ())), preferred_element_type=jnp.float32)

    return one(a[0], b[0]) + (one(a[0], b[1]) + one(a[1], b[0]))


VMEM_KIB = 52400


def kernel(nep, ndp, slots, *refs):
    old_ref, new_ref, counts_ref, acts_hbm, grads_hbm, w_hbm, master_hbm, one_hbm, two_hbm = refs[:9]
    out_ref, ig_ref, nm_ref, no_ref, nt_ref = refs[9:14]
    ns_refs = refs[14:14 + slots]
    (
        acts_all, g_in, g_mask, g_send, g_cols, w_all, grad_send, arrived,
        master, one, two, pick_send, pick_recv, out_v, ig_v,
        load_sem, store_sem,
        act_send_sem, act_recv_sem, w_send_sem, w_recv_sem, gs_sem, gr_sem,
        es_sem, er_sem, ps_sem, pr_sem,
    ) = refs[14 + slots:]
    ep = lax.axis_index("ep")
    dp = lax.axis_index("dp")
    half = ndp // 2
    sides, _, _, toks, width = acts_all.shape
    cols = w_all.shape[3]
    experts, rows, _ = master.shape
    _, chunks, _, crows, _ = grad_send.shape
    owners = nep // sides
    partner = dp + 1 - 2 * lax.rem(dp, 2)
    near = ep // owners
    quarter = ep // max(nep // 4, 1)
    outer = jnp.where((quarter == 0) | (quarter == 3), 0, 1)
    order = [lax.rem(near + outer + n, sides) for n in range(sides)]
    first = [jnp.where(side == near, 1, 0) for side in order]

    def local(src, dst, sem):
        return pltpu.make_async_copy(src, dst, sem)

    def remote(src, dst, ssem, rsem, e, d):
        return pltpu.make_async_remote_copy(
            src_ref=src, dst_ref=dst, send_sem=ssem, recv_sem=rsem,
            device_id=(e, d), device_id_type=MESH)

    load_grads = local(grads_hbm, g_in, load_sem.at[0])
    load_w = local(w_hbm, w_all.at[dp], load_sem.at[1])
    load_opt = [local(src, dst, load_sem.at[2 + n]) for n, (src, dst) in
                enumerate(((master_hbm, master), (one_hbm, one), (two_hbm, two)))]
    load_acts = [local(acts_hbm.at[:, :, pl.ds(h * width, width)], acts_all.at[h, dp], load_sem.at[5 + h])
                 for h in range(sides)]
    load_grads.start()
    for c in load_acts:
        c.start()
    load_w.start()
    for c in load_opt:
        c.start()

    barrier = pltpu.get_barrier_semaphore()
    for k in range(1, ndp):
        pl.semaphore_signal(barrier, inc=1, device_id=(ep, lax.rem(dp + k, ndp)), device_id_type=MESH)

    @pl.loop(1, nep)
    def _(k):
        pl.semaphore_signal(barrier, inc=1, device_id=(lax.rem(ep + k, nep), dp), device_id_type=MESH)

    load_grads.wait()
    for s in range(slots):
        live = (lax.broadcasted_iota(jnp.int32, (toks, 1), 0) < counts_ref[s]).astype(jnp.float32)
        masked = g_in[s] * live
        g_mask[s] = masked
        for j in range(ndp):
            g_send[j, s] = masked[:, j * cols:(j + 1) * cols]
        g_cols[dp, s] = g_send[dp, s]
    for c in load_acts:
        c.wait()

    pl.semaphore_wait(barrier, nep + ndp - 2)

    def grad_copy(k, s):
        to = lax.rem(dp - k + ndp, ndp)
        return remote(g_send.at[to, s], g_cols.at[dp, s], gs_sem.at[k - 1, s], gr_sem.at[k - 1, s], ep, to)

    def grad_arrival(k, s):
        came = g_cols.at[lax.rem(dp + k, ndp), s]
        return remote(came, came, gs_sem.at[k - 1, s], gr_sem.at[k - 1, s], ep, partner)

    def block_copy(view, k, ssem, rsem):
        own = view(dp)
        to = partner if k == 0 else lax.rem(dp - 2 * k + ndp, ndp)
        return remote(own, own, ssem(k), rsem(k), ep, to)

    def block_arrival(view, k, ssem, rsem):
        if k == 0:
            came = view(partner)
        elif k < half:
            came = view(lax.rem(dp + 2 * k, ndp))
        else:
            came = view(lax.rem(partner + 2 * (k - half + 1), ndp))
        return remote(came, came, ssem(k), rsem(k), ep, partner)

    def block_relay(view, k, ssem, rsem):
        block = view(lax.rem(dp + 2 * k, ndp))
        return remote(block, block, ssem(half - 1 + k), rsem(half - 1 + k), ep, partner)

    def acts_kit(n, s):
        return (lambda i: acts_all.at[order[n], i, s],
                lambda k: act_send_sem.at[k, n, s], lambda k: act_recv_sem.at[k, n, s])

    def w_kit(s):
        return (lambda i: w_all.at[i, s], lambda k: w_send_sem.at[k, s], lambda k: w_recv_sem.at[k, s])

    def send_block(view, ssem, rsem):
        for k in range(half - 1, -1, -1):
            block_copy(view, k, ssem, rsem).start()

    def relay_block(view, ssem, rsem):
        for k in range(1, half):
            block_arrival(view, k, ssem, rsem).wait_recv()
            block_relay(view, k, ssem, rsem).start()

    def finish_block(view, ssem, rsem):
        block_arrival(view, 0, ssem, rsem).wait_recv()
        for k in range(half, ndp - 1):
            block_arrival(view, k, ssem, rsem).wait_recv()

    pieces = [(n, s) for n in range(sides) for s in range(slots)]
    for n, s in pieces:
        if n == 0:
            for k in range(ndp - 1, 0, -1):
                grad_copy(k, s).start()
        send_block(*acts_kit(n, s))
    load_w.wait()
    for s in range(slots):
        send_block(*w_kit(s))

    def send_grad(n, s, c):
        base = order[n] * owners

        @pl.loop(first[n], owners)
        def _(k):
            to = base + lax.rem(ep + k, owners)
            remote(grad_send.at[s, c, to], arrived.at[s, c, ep], es_sem.at[s, c], er_sem.at[s, c], to, dp).start()

    for n, s in pieces:
        relay_block(*acts_kit(n, s))
        if n == 0:
            for k in range(1, ndp):
                grad_arrival(k, s).wait_recv()
        finish_block(*acts_kit(n, s))
        left = split(acts_all[order[n], :, s].reshape(ndp * toks, width))
        right = split(g_cols[:, s].reshape(ndp * toks, cols))
        grad = dot3(left, right, ((0,), (0,)))
        base = order[n] * owners
        for i in range(owners):
            for c in range(chunks):
                at = i * rows + c * crows
                grad_send[s, c, base + i] = grad[at:at + crows]
        send_grad(n, s, 0)
        if (n, s) == pieces[0]:
            for c in range(1, chunks):
                send_grad(n, s, c)
    for c in range(1, chunks):
        for n, s in pieces[1:]:
            send_grad(n, s, c)
    for s in range(slots):
        for c in range(chunks):
            arrived[s, c, ep] = grad_send[s, c, ep]

    for c in load_opt:
        c.wait()

    direct = rows % 8 == 0

    def landing(s, c, i):
        if direct:
            return ns_refs[s].at[pl.ds(pl.multiple_of(i * rows + c * crows, 8), crows)]
        return pick_recv.at[s, i]

    own_stores = []
    for c in range(chunks):
        for s in range(slots):
            came = arrived.at[s, c, pl.ds(0, nep - 1)]
            remote(came, came, es_sem.at[s, c], er_sem.at[s, c], ep, partner).wait_recv()
        span = slice(c * crows, (c + 1) * crows)

        @pl.loop(0, experts)
        def _(e):
            total = jnp.zeros((crows, cols), jnp.float32)
            for i in range(nep):
                for s in range(slots):
                    held = jnp.where(old_ref[i * slots + s] == e, 1.0, 0.0)
                    total = total + held * arrived[s, c, i]
            master[e, span], one[e, span], two[e, span] = adamw(
                master[e, span], one[e, span], two[e, span], total)

        def send_pick(to):
            for s in range(slots):
                pick_send[s, c, to] = master[new_ref[to * slots + s], span]
            for s in range(slots):
                remote(pick_send.at[s, c, to], landing(s, c, ep), ps_sem.at[s, c], pr_sem.at[s, c], to, dp).start()

        for n in range(sides):
            base = order[n] * owners

            @pl.loop(first[n], owners)
            def _(k):
                send_pick(base + lax.rem(ep + k, owners))

        for s in range(slots):
            pick_send[s, c, ep] = master[new_ref[ep * slots + s], span]
            own_stores.append(local(pick_send.at[s, c, ep], landing(s, c, ep), store_sem.at[5 + s, c]))
            own_stores[-1].start()

    stores = [local(src, dst, store_sem.at[n, 0]) for n, (src, dst) in
              enumerate(((master, nm_ref), (one, no_ref), (two, nt_ref)))]
    for c in stores:
        c.start()

    for s in range(slots):
        relay_block(*w_kit(s))
    last = []
    for s in range(slots):
        finish_block(*w_kit(s))
        live = (lax.broadcasted_iota(jnp.int32, (toks, 1), 0) < counts_ref[s]).astype(jnp.float32)
        acts = [split(acts_all[h, dp, s] * live) for h in range(sides)]
        back = [jnp.zeros((toks, width), jnp.float32) for h in range(sides)]
        for j in range(ndp):
            at = slice(j * cols, (j + 1) * cols)
            grads = split(g_mask[s, :, at])
            total = jnp.zeros((toks, cols), jnp.float32)
            for h in range(sides):
                weights = split(w_all[j, s, h * width:(h + 1) * width])
                total = total + dot3(acts[h], weights, ((1,), (0,)))
                back[h] = back[h] + dot3(grads, weights, ((1,), (1,)))
            out_v[s, :, at] = total
        for h in range(sides):
            ig_v[s, :, h * width:(h + 1) * width] = back[h]
    last = [local(out_v, out_ref, store_sem.at[3, 0]), local(ig_v, ig_ref, store_sem.at[4, 0])]
    for c in last:
        c.start()

    for n, s in pieces:
        if n == 0:
            for k in range(1, ndp):
                grad_copy(k, s).wait_send()
        for kit in [acts_kit(n, s)] + ([w_kit(s)] if n == 0 else []):
            for k in range(half):
                block_copy(kit[0], k, *kit[1:]).wait_send()
            for k in range(1, half):
                block_relay(kit[0], k, *kit[1:]).wait_send()
    for s in range(slots):
        for c in range(chunks):
            gone = grad_send.at[s, c, pl.ds(0, nep - 1)]
            remote(gone, gone, es_sem.at[s, c], er_sem.at[s, c], ep, partner).wait_send()
            gone = pick_send.at[s, c, pl.ds(0, nep - 1)]
            remote(gone, gone, ps_sem.at[s, c], pr_sem.at[s, c], ep, partner).wait_send()
    for c in own_stores + stores + last:
        c.wait()
    for s in range(slots):
        for c in range(chunks):
            if direct:
                came = ns_refs[s].at[pl.ds(0, (nep - 1) * crows)]
            else:
                came = pick_recv.at[s, pl.ds(0, nep - 1)]
            remote(came, came, ps_sem.at[s, c], pr_sem.at[s, c], ep, partner).wait_recv()
    if not direct:
        for s in range(slots):
            for i in range(nep):
                w_all[0, s, i * rows:(i + 1) * rows] = pick_recv[s, i]
            done = local(w_all.at[0, s], ns_refs[s], store_sem.at[0, 0])
            done.start()
            done.wait()


def write_out(slots, *refs):
    ins, outs, sems = refs[:5 + slots], refs[5 + slots:-1], refs[-1]
    parts = list(outs[:5]) + [outs[5].at[n] for n in range(slots)]
    copies = [pltpu.make_async_copy(src, dst, sems.at[n]) for n, (src, dst) in enumerate(zip(ins, parts))]
    for c in copies:
        c.start()
    for c in copies:
        c.wait()


def local_step(nep, ndp, activations, out_grads, counts, slot_weights, master, moment_one, moment_two, old_table, new_table):
    f32 = jnp.float32
    slots, toks, ff = activations.shape
    ds = out_grads.shape[2]
    cols = slot_weights.shape[2]
    experts, rows, _ = master.shape
    direct = rows % 8 == 0
    sides = 2
    chunks = 2 if rows % 16 == 0 else 1
    parted = (slots, chunks, nep, rows // chunks, cols)
    hbm = pl.BlockSpec(memory_space=pl.ANY)
    smem = pl.BlockSpec(memory_space=pltpu.SMEM)
    dma = pltpu.SemaphoreType.DMA
    shapes = [
        jax.ShapeDtypeStruct(x.shape, f32)
        for x in (out_grads, activations, master, moment_one, moment_two, slot_weights)
    ]
    results = pl.pallas_call(
        functools.partial(kernel, nep, ndp, slots),
        out_shape=shapes[:5] + [jax.ShapeDtypeStruct((ff, cols), f32)] * slots,
        in_specs=[smem] * 3 + [hbm] * 6,
        out_specs=[hbm] * (5 + slots),
        scratch_shapes=[
            pltpu.VMEM((sides, ndp, slots, toks, ff // sides), f32),
            pltpu.VMEM((slots, toks, ds), f32),
            pltpu.VMEM((slots, toks, ds), f32),
            pltpu.VMEM((ndp, slots, toks, cols), f32),
            pltpu.VMEM((ndp, slots, toks, cols), f32),
            pltpu.VMEM((ndp, slots, ff, cols), f32),
            pltpu.VMEM(parted, f32),
            pltpu.VMEM(parted, f32),
            pltpu.VMEM((experts, rows, cols), f32),
            pltpu.VMEM((experts, rows, cols), f32),
            pltpu.VMEM((experts, rows, cols), f32),
            pltpu.VMEM(parted, f32),
            pltpu.VMEM((1, 1, 8, 128) if direct else (slots, nep, rows, cols), f32),
            pltpu.VMEM((slots, toks, ds), f32),
            pltpu.VMEM((slots, toks, ff), f32),
            dma((5 + sides,)),
            dma((5 + slots, chunks)),
            dma((ndp - 1, sides, slots)),
            dma((ndp - 1, sides, slots)),
            dma((ndp - 1, slots)),
            dma((ndp - 1, slots)),
            dma((ndp - 1, slots)),
            dma((ndp - 1, slots)),
            dma((slots, chunks)),
            dma((slots, chunks)),
            dma((slots, chunks)),
            dma((slots, chunks)),
        ],
        compiler_params=pltpu.CompilerParams(
            collective_id=0, has_side_effects=True, vmem_limit_bytes=VMEM_KIB * 1024
        ),
        name="step",
    )(old_table.reshape(-1), new_table.reshape(-1), counts.reshape(-1), activations, out_grads, slot_weights, master, moment_one, moment_two)
    return pl.pallas_call(
        functools.partial(write_out, slots),
        out_shape=shapes,
        in_specs=[hbm] * (5 + slots),
        out_specs=[hbm] * 6,
        scratch_shapes=[dma((5 + slots,))],
        compiler_params=pltpu.CompilerParams(vmem_limit_bytes=1024 * 1024),
        name="write_out",
    )(*results)


def solution(mesh):
    in_specs = (
        P("ep", "dp", None),
        P("ep", "dp", None),
        P("ep", "dp"),
        P("ep", None, "dp"),
        P(None, "ep", "dp"),
        P(None, "ep", "dp"),
        P(None, "ep", "dp"),
        P(),
        P(),
    )
    out_specs = (
        P("ep", "dp", None),
        P("ep", "dp", None),
        P(None, "ep", "dp"),
        P(None, "ep", "dp"),
        P(None, "ep", "dp"),
        P("ep", None, "dp"),
    )
    step = functools.partial(local_step, mesh.shape["ep"], mesh.shape["dp"])
    return jax.shard_map(step, mesh=mesh, in_specs=in_specs, out_specs=out_specs, check_vma=False)
```

profile of v0, /device:TPU:0, one launch (start us, length us, event | category | flops | bytes accessed | tf_op | source)
XLA Modules:
  0.0 54.3 jit_solution(11381409665267344980)
XLA Ops:
  0.6 0.0 copy-start.1
  0.6 0.0 copy-start.2
  0.7 0.0 copy-start.3
  0.7 0.6 %copy-done.1 = s32[16,1]{0,1:T(1,128)S(1)} copy-done((s32[16,1]{0,1:T(1,128)S(1)}, s32[16,1]{0,1:T(1,128)}, u32[]{:S(2)}) %copy-start.1) | copy-done | bytes 88
  1.3 0.0 copy-done.2
  1.3 0.0 copy-done.3
  1.3 0.0 copy-start
  1.3 0.9 %copy-done = f32[2,64,512]{2,1,0:T(8,128)S(1)} copy-done((f32[2,64,512]{2,1,0:T(8,128)S(1)}, f32[2,64,512]{2,1,0:T(8,128)}, u32[]{:S(2)}) %copy-start) | copy-done | bytes 262168
  2.3 50.5 %step.1 = (f32[2,64,512]{2,1,0:T(8,128)S(1)}, f32[2,64,768]{2,1,0:T(8,128)S(1)}, f32[8,96,128]{2,1,0:T(8,128)S(1)}, f32[8,96,128]{2,1,0:T(8,128)S(1)}, f32[8,96,...) custom-call(s32[16]{0:T(128)S(1)} %bitcast.3, s32[16]{0:T(128)S(1)} %bitcast.4, s32[2]{0:T(128)S(1)} %bitcast.5, ...), custom_call_target="tpu_custom_call" | custom-call | tf_op jit(solution)/shard_map/step/pallas_call | solution.py:338
  52.8 1.5 %write_out.1 = (f32[2,64,512]{2,1,0:T(8,128)}, f32[2,64,768]{2,1,0:T(8,128)}, f32[8,96,128]{2,1,0:T(8,128)}, f32[8,96,128]{2,1,0:T(8,128)}, f32[8,96,128]{2,1,0:T(8,128)}, /*index=5*/f32[2,768,128]{2,1,0:T(8,128)}) custom-call(f32[2,64,512]{2,1,0:T(8,128)S(1)} %get-tuple-element.13.refs_0_, f32[2,64,768]{2,1,0:T(8,128)S(1)} %get-tuple-element.14.refs_1_, ...), custom_call_target="tpu_custom_call" | custom-call | tf_op jit(solution)/shard_map/write_out/pallas_call | solution.py:377
Async XLA Ops:
  0.6 0.7 %copy-start.1 = (s32[16,1]{0,1:T(1,128)S(1)}, s32[16,1]{0,1:T(1,128)}, u32[]{:S(2)}) copy-start(s32[16,1]{0,1:T(1,128)} %param.16) | copy-start | bytes 196
  0.6 0.7 %copy-start.2 = (s32[16,1]{0,1:T(1,128)S(1)}, s32[16,1]{0,1:T(1,128)}, u32[]{:S(2)}) copy-start(s32[16,1]{0,1:T(1,128)} %param.17) | copy-start | bytes 196
  0.7 0.7 %copy-start.3 = (s32[2,1]{0,1:T(1,128)S(1)}, s32[2,1]{0,1:T(1,128)}, u32[]{:S(2)}) copy-start(s32[2,1]{0,1:T(1,128)} %param.11) | copy-start | bytes 28
  1.3 0.9 %copy-start = (f32[2,64,512]{2,1,0:T(8,128)S(1)}, f32[2,64,512]{2,1,0:T(8,128)}, u32[]{:S(2)}) copy-start(f32[2,64,512]{2,1,0:T(8,128)} %refs_4_.1) | copy-start | bytes 786436
where the time goes:
time: 54.5 us; the launch traced here: 54.3 us
  Pallas kernels  52 us (95%)
  local copies, waits for them, and re-layouts  1.61 us (3%)
  between operations  0.67 us (1%)
    pallas_call x1, Pallas kernels, local_step(): pl.pallas_call(functools.partial(kernel, nep, ndp, slots), out_shape=shap...  50.5 us
    unnamed x8, local copies, waits for them, and re-layouts  1.61 us
    pallas_call x1, Pallas kernels, local_step(): pl.pallas_call(functools.partial(write_out, slots), out_shape=shapes, in_...  1.54 us

commit v1 on v0

--- a/solution.py
+++ b/solution.py
@@ -44,13 +44,24 @@
 VMEM_KIB = 52400
 
 
+def piece_blocks(sides, slots, width):
+    step = 128 if width % 128 == 0 else width
+    found = []
+    for n in range(sides):
+        for s in range(slots):
+            size = step if n == 0 and s == 0 else width
+            found += [(n, s, low, low + size) for low in range(0, width, size)]
+    return found
+
+
 def kernel(nep, ndp, slots, *refs):
-    old_ref, new_ref, counts_ref, acts_hbm, grads_hbm, w_hbm, master_hbm, one_hbm, two_hbm = refs[:9]
+    old_hbm, new_hbm, counts_hbm, acts_hbm, grads_hbm, w_hbm, master_hbm, one_hbm, two_hbm = refs[:9]
     out_ref, ig_ref, nm_ref, no_ref, nt_ref = refs[9:14]
     ns_refs = refs[14:14 + slots]
     (
         acts_all, g_in, g_mask, g_send, g_cols, w_all, grad_send, arrived,
         master, one, two, pick_send, pick_recv, out_v, ig_v,
+        old_ref, new_ref, counts_ref, table_sem, joined, opened,
         load_sem, store_sem,
         act_send_sem, act_recv_sem, w_send_sem, w_recv_sem, gs_sem, gr_sem,
         es_sem, er_sem, ps_sem, pr_sem,
@@ -78,39 +89,60 @@
             src_ref=src, dst_ref=dst, send_sem=ssem, recv_sem=rsem,
             device_id=(e, d), device_id_type=MESH)
 
+    tables = [local(src, dst, table_sem.at[n]) for n, (src, dst) in
+              enumerate(((counts_hbm, counts_ref), (old_hbm, old_ref), (new_hbm, new_ref)))]
     load_grads = local(grads_hbm, g_in, load_sem.at[0])
     load_w = local(w_hbm, w_all.at[dp], load_sem.at[1])
     load_opt = [local(src, dst, load_sem.at[2 + n]) for n, (src, dst) in
                 enumerate(((master_hbm, master), (one_hbm, one), (two_hbm, two)))]
     load_acts = [local(acts_hbm.at[:, :, pl.ds(h * width, width)], acts_all.at[h, dp], load_sem.at[5 + h])
                  for h in range(sides)]
+    tables[0].start()
+    for c in load_acts:
+        c.start()
     load_grads.start()
-    for c in load_acts:
+    for c in tables[1:]:
         c.start()
     load_w.start()
     for c in load_opt:
         c.start()
 
+    gate = ndp - 1
     barrier = pltpu.get_barrier_semaphore()
     for k in range(1, ndp):
-        pl.semaphore_signal(barrier, inc=1, device_id=(ep, lax.rem(dp + k, ndp)), device_id_type=MESH)
-
-    @pl.loop(1, nep)
-    def _(k):
-        pl.semaphore_signal(barrier, inc=1, device_id=(lax.rem(ep + k, nep), dp), device_id_type=MESH)
-
-    load_grads.wait()
-    for s in range(slots):
-        live = (lax.broadcasted_iota(jnp.int32, (toks, 1), 0) < counts_ref[s]).astype(jnp.float32)
-        masked = g_in[s] * live
-        g_mask[s] = masked
-        for j in range(ndp):
-            g_send[j, s] = masked[:, j * cols:(j + 1) * cols]
-        g_cols[dp, s] = g_send[dp, s]
-    for c in load_acts:
-        c.wait()
-
-    pl.semaphore_wait(barrier, nep + ndp - 2)
+        to = lax.rem(dp + k, ndp)
+
+        @pl.when(to != gate)
+        def _():
+            pl.semaphore_signal(barrier, inc=1, device_id=(ep, to), device_id_type=MESH)
+
+    @pl.when(dp != gate)
+    def _():
+        pl.semaphore_wait(barrier, ndp - 1)
+
+    @pl.when(dp == gate - 1)
+    def _():
+        pl.semaphore_signal(joined, inc=1, device_id=(ep, gate), device_id_type=MESH)
+
+    @pl.when(dp == gate)
+    def _():
+        pl.semaphore_wait(joined, 1)
+
+        @pl.loop(1, nep)
+        def _(k):
+            pl.semaphore_signal(barrier, inc=1, device_id=(lax.rem(ep + k, nep), gate), device_id_type=MESH)
+
+    def open_gate():
+        @pl.when(dp == gate)
+        def _():
+            pl.semaphore_wait(barrier, nep - 1)
+            for j in range(gate):
+                pl.semaphore_signal(opened, inc=1, device_id=(ep, j), device_id_type=MESH)
+
+    def pass_gate():
+        @pl.when(dp != gate)
+        def _():
+            pl.semaphore_wait(opened, 1)
 
     def grad_copy(k, s):
         to = lax.rem(dp - k + ndp, ndp)
@@ -138,9 +170,10 @@
         block = view(lax.rem(dp + 2 * k, ndp))
         return remote(block, block, ssem(half - 1 + k), rsem(half - 1 + k), ep, partner)
 
-    def acts_kit(n, s):
-        return (lambda i: acts_all.at[order[n], i, s],
-                lambda k: act_send_sem.at[k, n, s], lambda k: act_recv_sem.at[k, n, s])
+    def acts_kit(b):
+        n, s, low, high = blocks[b]
+        return (lambda i: acts_all.at[order[n], i, s, :, pl.ds(low, high - low)],
+                lambda k: act_send_sem.at[k, b], lambda k: act_recv_sem.at[k, b])
 
     def w_kit(s):
         return (lambda i: w_all.at[i, s], lambda k: w_send_sem.at[k, s], lambda k: w_recv_sem.at[k, s])
@@ -160,11 +193,29 @@
             block_arrival(view, k, ssem, rsem).wait_recv()
 
     pieces = [(n, s) for n in range(sides) for s in range(slots)]
-    for n, s in pieces:
-        if n == 0:
-            for k in range(ndp - 1, 0, -1):
-                grad_copy(k, s).start()
-        send_block(*acts_kit(n, s))
+    blocks = piece_blocks(sides, slots, width)
+
+    for c in load_acts:
+        c.wait()
+    send_block(*acts_kit(0))
+    tables[0].wait()
+    load_grads.wait()
+    for s in range(slots):
+        live = (lax.broadcasted_iota(jnp.int32, (toks, 1), 0) < counts_ref[s]).astype(jnp.float32)
+        masked = g_in[s] * live
+        g_mask[s] = masked
+        for j in range(ndp):
+            g_send[j, s] = masked[:, j * cols:(j + 1) * cols]
+        g_cols[dp, s] = g_send[dp, s]
+        for k in range(ndp - 1, 0, -1):
+            grad_copy(k, s).start()
+        if s == 0:
+            for b, (n, t, _, _) in enumerate(blocks):
+                if b and (n, t) == pieces[0]:
+                    send_block(*acts_kit(b))
+    for b, (n, s, _, _) in enumerate(blocks):
+        if (n, s) != pieces[0]:
+            send_block(*acts_kit(b))
     load_w.wait()
     for s in range(slots):
         send_block(*w_kit(s))
@@ -177,24 +228,43 @@
             to = base + lax.rem(ep + k, owners)
             remote(grad_send.at[s, c, to], arrived.at[s, c, ep], es_sem.at[s, c], er_sem.at[s, c], to, dp).start()
 
-    for n, s in pieces:
-        relay_block(*acts_kit(n, s))
-        if n == 0:
+    def send_some(n, s, start, stop):
+        base = order[n] * owners
+
+        @pl.loop(start, stop)
+        def _(i):
+            to = base + i
+
+            @pl.when(to != ep)
+            def _():
+                for c in range(chunks):
+                    remote(grad_send.at[s, c, to], arrived.at[s, c, ep], es_sem.at[s, c], er_sem.at[s, c], to, dp).start()
+
+    rights = {}
+    for b, (n, s, low, high) in enumerate(blocks):
+        relay_block(*acts_kit(b))
+        if b == 0:
+            open_gate()
+        if s not in rights:
             for k in range(1, ndp):
                 grad_arrival(k, s).wait_recv()
-        finish_block(*acts_kit(n, s))
-        left = split(acts_all[order[n], :, s].reshape(ndp * toks, width))
-        right = split(g_cols[:, s].reshape(ndp * toks, cols))
-        grad = dot3(left, right, ((0,), (0,)))
+            rights[s] = split(g_cols[:, s].reshape(ndp * toks, cols))
+        finish_block(*acts_kit(b))
+        left = split(acts_all[order[n], :, s, :, low:high].reshape(ndp * toks, high - low))
+        grad = dot3(left, rights[s], ((0,), (0,)))
         base = order[n] * owners
         for i in range(owners):
             for c in range(chunks):
                 at = i * rows + c * crows
-                grad_send[s, c, base + i] = grad[at:at + crows]
-        send_grad(n, s, 0)
+                start, stop = max(at, low), min(at + crows, high)
+                if start < stop:
+                    grad_send[s, c, base + i, start - at:stop - at] = grad[start - low:stop - low]
+        if b == 0:
+            pass_gate()
         if (n, s) == pieces[0]:
-            for c in range(1, chunks):
-                send_grad(n, s, c)
+            send_some(n, s, low // rows, high // rows)
+        else:
+            send_grad(n, s, 0)
     for c in range(1, chunks):
         for n, s in pieces[1:]:
             send_grad(n, s, c)
@@ -202,7 +272,7 @@
         for c in range(chunks):
             arrived[s, c, ep] = grad_send[s, c, ep]
 
-    for c in load_opt:
+    for c in tables[1:] + load_opt:
         c.wait()
 
     direct = rows % 8 == 0
@@ -275,15 +345,14 @@
     for c in last:
         c.start()
 
-    for n, s in pieces:
-        if n == 0:
-            for k in range(1, ndp):
-                grad_copy(k, s).wait_send()
-        for kit in [acts_kit(n, s)] + ([w_kit(s)] if n == 0 else []):
-            for k in range(half):
-                block_copy(kit[0], k, *kit[1:]).wait_send()
-            for k in range(1, half):
-                block_relay(kit[0], k, *kit[1:]).wait_send()
+    for s in range(slots):
+        for k in range(1, ndp):
+            grad_copy(k, s).wait_send()
+    for kit in [acts_kit(b) for b in range(len(blocks))] + [w_kit(s) for s in range(slots)]:
+        for k in range(half):
+            block_copy(kit[0], k, *kit[1:]).wait_send()
+        for k in range(1, half):
+            block_relay(kit[0], k, *kit[1:]).wait_send()
     for s in range(slots):
         for c in range(chunks):
             gone = grad_send.at[s, c, pl.ds(0, nep - 1)]
@@ -327,9 +396,9 @@
     direct = rows % 8 == 0
     sides = 2
     chunks = 2 if rows % 16 == 0 else 1
+    blocks = len(piece_blocks(sides, slots, ff // sides))
     parted = (slots, chunks, nep, rows // chunks, cols)
     hbm = pl.BlockSpec(memory_space=pl.ANY)
-    smem = pl.BlockSpec(memory_space=pltpu.SMEM)
     dma = pltpu.SemaphoreType.DMA
     shapes = [
         jax.ShapeDtypeStruct(x.shape, f32)
@@ -338,7 +407,7 @@
     results = pl.pallas_call(
         functools.partial(kernel, nep, ndp, slots),
         out_shape=shapes[:5] + [jax.ShapeDtypeStruct((ff, cols), f32)] * slots,
-        in_specs=[smem] * 3 + [hbm] * 6,
+        in_specs=[hbm] * 9,
         out_specs=[hbm] * (5 + slots),
         scratch_shapes=[
             pltpu.VMEM((sides, ndp, slots, toks, ff // sides), f32),
@@ -356,10 +425,16 @@
             pltpu.VMEM((1, 1, 8, 128) if direct else (slots, nep, rows, cols), f32),
             pltpu.VMEM((slots, toks, ds), f32),
             pltpu.VMEM((slots, toks, ff), f32),
+            pltpu.SMEM((nep * slots,), jnp.int32),
+            pltpu.SMEM((nep * slots,), jnp.int32),
+            pltpu.SMEM((slots,), jnp.int32),
+            dma((3,)),
+            pltpu.SemaphoreType.REGULAR,
+            pltpu.SemaphoreType.REGULAR,
             dma((5 + sides,)),
             dma((5 + slots, chunks)),
-            dma((ndp - 1, sides, slots)),
-            dma((ndp - 1, sides, slots)),
+            dma((ndp - 1, blocks)),
+            dma((ndp - 1, blocks)),
             dma((ndp - 1, slots)),
             dma((ndp - 1, slots)),
             dma((ndp - 1, slots)),
@@ -373,7 +448,9 @@
             collective_id=0, has_side_effects=True, vmem_limit_bytes=VMEM_KIB * 1024
         ),
         name="step",
-    )(old_table.reshape(-1), new_table.reshape(-1), counts.reshape(-1), activations, out_grads, slot_weights, master, moment_one, moment_two)
+    )(*[pltpu.with_memory_space_constraint(x, pltpu.HBM) for x in (
+        old_table.reshape(-1), new_table.reshape(-1), counts.reshape(-1),
+        activations, out_grads, slot_weights, master, moment_one, moment_two)])
     return pl.pallas_call(
         functools.partial(write_out, slots),
         out_shape=shapes,

time: 54.5 us -> 52.4 us (0.961)
  local copies, waits for them, and re-layouts: 1.61 us -> 0 us
    unnamed x8 -> x0, local copies, waits for them, and re-layouts: 1.61 us -> none
where the time goes in v1:
time: 52.4 us; the launch traced here: 52.3 us
  Pallas kernels  51.6 us (98%)
  between operations  0.64 us (1%)
    pallas_call x1, Pallas kernels, local_step(): pl.pallas_call(functools.partial(kernel, nep, ndp, slots), out_shape=shap...  50.1 us
    pallas_call x1, Pallas kernels, local_step(): pl.pallas_call(functools.partial(write_out, slots), out_shape=shapes, in_...  1.54 us

profile of v1, /device:TPU:0, one launch (start us, length us, event | category | flops | bytes accessed | tf_op | source)
XLA Modules:
  0.0 52.3 jit_solution(12459172348021640609)
XLA Ops:
  0.6 50.1 %step.1 = (f32[2,64,512]{2,1,0:T(8,128)S(1)}, f32[2,64,768]{2,1,0:T(8,128)S(1)}, f32[8,96,128]{2,1,0:T(8,128)S(1)}, f32[8,96,128]{2,1,0:T(8,128)S(1)}, f32[8,96,...) custom-call(s32[16]{0:T(128)} %bitcast.3, s32[16]{0:T(128)} %bitcast.4, s32[2]{0:T(128)} %bitcast.5, ...), custom_call_target="tpu_custom_call" | custom-call | tf_op jit(solution)/shard_map/step/pallas_call | solution.py:407
  50.7 1.5 %write_out.1 = (f32[2,64,512]{2,1,0:T(8,128)}, f32[2,64,768]{2,1,0:T(8,128)}, f32[8,96,128]{2,1,0:T(8,128)}, f32[8,96,128]{2,1,0:T(8,128)}, f32[8,96,128]{2,1,0:T(8,128)}, /*index=5*/f32[2,768,128]{2,1,0:T(8,128)}) custom-call(f32[2,64,512]{2,1,0:T(8,128)S(1)} %get-tuple-element.13.refs_0_, f32[2,64,768]{2,1,0:T(8,128)S(1)} %get-tuple-element.14.refs_1_, ...), custom_call_target="tpu_custom_call" | custom-call | tf_op jit(solution)/shard_map/write_out/pallas_call | solution.py:454

commit v2 on v1

--- a/solution.py
+++ b/solution.py
@@ -80,6 +80,8 @@
     outer = jnp.where((quarter == 0) | (quarter == 3), 0, 1)
     order = [lax.rem(near + outer + n, sides) for n in range(sides)]
     first = [jnp.where(side == near, 1, 0) for side in order]
+    away = [lax.rem(near + 1 + n, sides) for n in range(sides)]
+    skip = [0] * (sides - 1) + [1]
 
     def local(src, dst, sem):
         return pltpu.make_async_copy(src, dst, sem)
@@ -172,7 +174,7 @@
 
     def acts_kit(b):
         n, s, low, high = blocks[b]
-        return (lambda i: acts_all.at[order[n], i, s, :, pl.ds(low, high - low)],
+        return (lambda i: acts_all.at[away[n], i, s, :, pl.ds(low, high - low)],
                 lambda k: act_send_sem.at[k, b], lambda k: act_recv_sem.at[k, b])
 
     def w_kit(s):
@@ -221,15 +223,15 @@
         send_block(*w_kit(s))
 
     def send_grad(n, s, c):
-        base = order[n] * owners
-
-        @pl.loop(first[n], owners)
+        base = away[n] * owners
+
+        @pl.loop(skip[n], owners)
         def _(k):
             to = base + lax.rem(ep + k, owners)
             remote(grad_send.at[s, c, to], arrived.at[s, c, ep], es_sem.at[s, c], er_sem.at[s, c], to, dp).start()
 
     def send_some(n, s, start, stop):
-        base = order[n] * owners
+        base = away[n] * owners
 
         @pl.loop(start, stop)
         def _(i):
@@ -250,9 +252,9 @@
                 grad_arrival(k, s).wait_recv()
             rights[s] = split(g_cols[:, s].reshape(ndp * toks, cols))
         finish_block(*acts_kit(b))
-        left = split(acts_all[order[n], :, s, :, low:high].reshape(ndp * toks, high - low))
+        left = split(acts_all[away[n], :, s, :, low:high].reshape(ndp * toks, high - low))
         grad = dot3(left, rights[s], ((0,), (0,)))
-        base = order[n] * owners
+        base = away[n] * owners
         for i in range(owners):
             for c in range(chunks):
                 at = i * rows + c * crows

time: 52.4 us -> 49.2 us (0.939)
  Pallas kernels: 51.6 us -> 48.4 us
    pallas_call x1, Pallas kernels: 50.1 us -> 46.8 us  [local_step(): pl.pallas_call(functools.partial(kernel, nep, ndp, slots), out_shape=shap...]
where the time goes in v2:
time: 49.2 us; the launch traced here: 49 us
  Pallas kernels  48.4 us (98%)
  between operations  0.64 us (1%)
    pallas_call x1, Pallas kernels, local_step(): pl.pallas_call(functools.partial(kernel, nep, ndp, slots), out_shape=shap...  46.8 us
    pallas_call x1, Pallas kernels, local_step(): pl.pallas_call(functools.partial(write_out, slots), out_shape=shapes, in_...  1.54 us

profile of v2, /device:TPU:0, one launch (start us, length us, event | category | flops | bytes accessed | tf_op | source)
XLA Modules:
  0.0 49.0 jit_solution(14293568426850955876)
XLA Ops:
  0.6 46.8 %step.1 = (f32[2,64,512]{2,1,0:T(8,128)S(1)}, f32[2,64,768]{2,1,0:T(8,128)S(1)}, f32[8,96,128]{2,1,0:T(8,128)S(1)}, f32[8,96,128]{2,1,0:T(8,128)S(1)}, f32[8,96,...) custom-call(s32[16]{0:T(128)} %bitcast.3, s32[16]{0:T(128)} %bitcast.4, s32[2]{0:T(128)} %bitcast.5, ...), custom_call_target="tpu_custom_call" | custom-call | tf_op jit(solution)/shard_map/step/pallas_call | solution.py:409
  47.5 1.5 %write_out.1 = (f32[2,64,512]{2,1,0:T(8,128)}, f32[2,64,768]{2,1,0:T(8,128)}, f32[8,96,128]{2,1,0:T(8,128)}, f32[8,96,128]{2,1,0:T(8,128)}, f32[8,96,128]{2,1,0:T(8,128)}, /*index=5*/f32[2,768,128]{2,1,0:T(8,128)}) custom-call(f32[2,64,512]{2,1,0:T(8,128)S(1)} %get-tuple-element.13.refs_0_, f32[2,64,768]{2,1,0:T(8,128)S(1)} %get-tuple-element.14.refs_1_, ...), custom_call_target="tpu_custom_call" | custom-call | tf_op jit(solution)/shard_map/write_out/pallas_call | solution.py:456

commit v3 on v2

--- a/solution.py
+++ b/solution.py
@@ -82,6 +82,15 @@
     first = [jnp.where(side == near, 1, 0) for side in order]
     away = [lax.rem(near + 1 + n, sides) for n in range(sides)]
     skip = [0] * (sides - 1) + [1]
+    place = lax.rem(ep, owners)
+
+    def target(n_side, k):
+        base = n_side * owners
+        up = base + owners - 1 - k
+        down = base + k
+        other = jnp.where(n_side > near, up, down)
+        mine = base + lax.rem(place + k, owners)
+        return jnp.where(n_side == near, mine, other)
 
     def local(src, dst, sem):
         return pltpu.make_async_copy(src, dst, sem)
@@ -223,11 +232,9 @@
         send_block(*w_kit(s))
 
     def send_grad(n, s, c):
-        base = away[n] * owners
-
         @pl.loop(skip[n], owners)
         def _(k):
-            to = base + lax.rem(ep + k, owners)
+            to = target(away[n], k)
             remote(grad_send.at[s, c, to], arrived.at[s, c, ep], es_sem.at[s, c], er_sem.at[s, c], to, dp).start()
 
     def send_some(n, s, start, stop):
@@ -308,11 +315,9 @@
                 remote(pick_send.at[s, c, to], landing(s, c, ep), ps_sem.at[s, c], pr_sem.at[s, c], to, dp).start()
 
         for n in range(sides):
-            base = order[n] * owners
-
             @pl.loop(first[n], owners)
             def _(k):
-                send_pick(base + lax.rem(ep + k, owners))
+                send_pick(target(order[n], k))
 
         for s in range(slots):
             pick_send[s, c, ep] = master[new_ref[ep * slots + s], span]

time: 49.2 us -> 46.4 us (0.943)
  Pallas kernels: 48.4 us -> 45.6 us
    pallas_call x1, Pallas kernels: 46.8 us -> 44.1 us  [local_step(): pl.pallas_call(functools.partial(kernel, nep, ndp, slots), out_shape=shap...]
where the time goes in v3:
time: 46.4 us; the launch traced here: 46.2 us
  Pallas kernels  45.6 us (98%)
  between operations  0.64 us (1%)
    pallas_call x1, Pallas kernels, local_step(): pl.pallas_call(functools.partial(kernel, nep, ndp, slots), out_shape=shap...  44.1 us
    pallas_call x1, Pallas kernels, local_step(): pl.pallas_call(functools.partial(write_out, slots), out_shape=shapes, in_...  1.54 us

profile of v3, /device:TPU:0, one launch (start us, length us, event | category | flops | bytes accessed | tf_op | source)
XLA Modules:
  0.0 46.2 jit_solution(3556514109593091778)
XLA Ops:
  0.6 44.1 %step.1 = (f32[2,64,512]{2,1,0:T(8,128)S(1)}, f32[2,64,768]{2,1,0:T(8,128)S(1)}, f32[8,96,128]{2,1,0:T(8,128)S(1)}, f32[8,96,128]{2,1,0:T(8,128)S(1)}, f32[8,96,...) custom-call(s32[16]{0:T(128)} %bitcast.3, s32[16]{0:T(128)} %bitcast.4, s32[2]{0:T(128)} %bitcast.5, ...), custom_call_target="tpu_custom_call" | custom-call | tf_op jit(solution)/shard_map/step/pallas_call | solution.py:414
  44.7 1.5 %write_out.1 = (f32[2,64,512]{2,1,0:T(8,128)}, f32[2,64,768]{2,1,0:T(8,128)}, f32[8,96,128]{2,1,0:T(8,128)}, f32[8,96,128]{2,1,0:T(8,128)}, f32[8,96,128]{2,1,0:T(8,128)}, /*index=5*/f32[2,768,128]{2,1,0:T(8,128)}) custom-call(f32[2,64,512]{2,1,0:T(8,128)S(1)} %get-tuple-element.13.refs_0_, f32[2,64,768]{2,1,0:T(8,128)S(1)} %get-tuple-element.14.refs_1_, ...), custom_call_target="tpu_custom_call" | custom-call | tf_op jit(solution)/shard_map/write_out/pallas_call | solution.py:461

commit v4 on v3

--- a/solution.py
+++ b/solution.py
@@ -1,4 +1,5 @@
 import functools
+import math
 
 import jax
 import jax.numpy as jnp
@@ -47,8 +48,8 @@
 def piece_blocks(sides, slots, width):
     step = 128 if width % 128 == 0 else width
     found = []
-    for n in range(sides):
-        for s in range(slots):
+    for s in range(slots):
+        for n in range(sides):
             size = step if n == 0 and s == 0 else width
             found += [(n, s, low, low + size) for low in range(0, width, size)]
     return found
@@ -102,21 +103,30 @@
 
     tables = [local(src, dst, table_sem.at[n]) for n, (src, dst) in
               enumerate(((counts_hbm, counts_ref), (old_hbm, old_ref), (new_hbm, new_ref)))]
-    load_grads = local(grads_hbm, g_in, load_sem.at[0])
-    load_w = local(w_hbm, w_all.at[dp], load_sem.at[1])
-    load_opt = [local(src, dst, load_sem.at[2 + n]) for n, (src, dst) in
+    load_grads = [local(grads_hbm.at[s], g_in.at[s], load_sem.at[s]) for s in range(slots)]
+    load_w = local(w_hbm, w_all.at[dp], load_sem.at[slots])
+    load_opt = [local(src, dst, load_sem.at[slots + 1 + n]) for n, (src, dst) in
                 enumerate(((master_hbm, master), (one_hbm, one), (two_hbm, two)))]
-    load_acts = [local(acts_hbm.at[:, :, pl.ds(h * width, width)], acts_all.at[h, dp], load_sem.at[5 + h])
-                 for h in range(sides)]
+    pieces = [(n, s) for s in range(slots) for n in range(sides)]
+    blocks = piece_blocks(sides, slots, width)
+
+    def load_block(b):
+        n, s, low, high = blocks[b]
+        start = pl.multiple_of(away[n] * width + low, math.gcd(width, 128))
+        return local(acts_hbm.at[s, :, pl.ds(start, high - low)], acts_all.at[away[n], dp, s, :, pl.ds(low, high - low)],
+                     load_sem.at[slots + 4 + b])
+
+    load_block(0).start()
     tables[0].start()
-    for c in load_acts:
+    load_grads[0].start()
+    for b in range(1, len(blocks)):
+        if blocks[b][:2] == pieces[0]:
+            load_block(b).start()
+    for c in load_grads[1:]:
         c.start()
-    load_grads.start()
-    for c in tables[1:]:
-        c.start()
-    load_w.start()
-    for c in load_opt:
-        c.start()
+    for b in range(1, len(blocks)):
+        if blocks[b][:2] != pieces[0]:
+            load_block(b).start()
 
     gate = ndp - 1
     barrier = pltpu.get_barrier_semaphore()
@@ -203,29 +213,30 @@
         for k in range(half, ndp - 1):
             block_arrival(view, k, ssem, rsem).wait_recv()
 
-    pieces = [(n, s) for n in range(sides) for s in range(slots)]
-    blocks = piece_blocks(sides, slots, width)
-
-    for c in load_acts:
-        c.wait()
+    load_block(0).wait()
     send_block(*acts_kit(0))
     tables[0].wait()
-    load_grads.wait()
-    for s in range(slots):
+    for s in range(slots):
+        load_grads[s].wait()
         live = (lax.broadcasted_iota(jnp.int32, (toks, 1), 0) < counts_ref[s]).astype(jnp.float32)
         masked = g_in[s] * live
-        g_mask[s] = masked
         for j in range(ndp):
             g_send[j, s] = masked[:, j * cols:(j + 1) * cols]
-        g_cols[dp, s] = g_send[dp, s]
         for k in range(ndp - 1, 0, -1):
             grad_copy(k, s).start()
         if s == 0:
-            for b, (n, t, _, _) in enumerate(blocks):
-                if b and (n, t) == pieces[0]:
+            for b in range(1, len(blocks)):
+                if blocks[b][:2] == pieces[0]:
+                    load_block(b).wait()
                     send_block(*acts_kit(b))
-    for b, (n, s, _, _) in enumerate(blocks):
-        if (n, s) != pieces[0]:
+            load_w.start()
+            for c in tables[1:] + load_opt:
+                c.start()
+        g_mask[s] = masked
+        g_cols[dp, s] = g_send[dp, s]
+    for b in range(1, len(blocks)):
+        if blocks[b][:2] != pieces[0]:
+            load_block(b).wait()
             send_block(*acts_kit(b))
     load_w.wait()
     for s in range(slots):
@@ -254,12 +265,12 @@
         relay_block(*acts_kit(b))
         if b == 0:
             open_gate()
+        finish_block(*acts_kit(b))
+        left = split(acts_all[away[n], :, s, :, low:high].reshape(ndp * toks, high - low))
         if s not in rights:
             for k in range(1, ndp):
                 grad_arrival(k, s).wait_recv()
             rights[s] = split(g_cols[:, s].reshape(ndp * toks, cols))
-        finish_block(*acts_kit(b))
-        left = split(acts_all[away[n], :, s, :, low:high].reshape(ndp * toks, high - low))
         grad = dot3(left, rights[s], ((0,), (0,)))
         base = away[n] * owners
         for i in range(owners):
@@ -438,7 +449,7 @@
             dma((3,)),
             pltpu.SemaphoreType.REGULAR,
             pltpu.SemaphoreType.REGULAR,
-            dma((5 + sides,)),
+            dma((slots + 4 + blocks,)),
             dma((5 + slots, chunks)),
             dma((ndp - 1, blocks)),
             dma((ndp - 1, blocks)),

time: 46.4 us -> 45.9 us (0.989)
  Pallas kernels: 45.6 us -> 45.1 us
    pallas_call x1, Pallas kernels: 44.1 us -> 43.6 us  [local_step(): pl.pallas_call(functools.partial(kernel, nep, ndp, slots), out_shape=shap...]
where the time goes in v4:
time: 45.9 us; the launch traced here: 45.8 us
  Pallas kernels  45.1 us (98%)
  between operations  0.64 us (1%)
    pallas_call x1, Pallas kernels, local_step(): pl.pallas_call(functools.partial(kernel, nep, ndp, slots), out_shape=shap...  43.6 us
    pallas_call x1, Pallas kernels, local_step(): pl.pallas_call(functools.partial(write_out, slots), out_shape=shapes, in_...  1.54 us

profile of v4, /device:TPU:0, one launch (start us, length us, event | category | flops | bytes accessed | tf_op | source)
XLA Modules:
  0.0 45.8 jit_solution(4052553909950302884)
XLA Ops:
  0.6 43.6 %step.1 = (f32[2,64,512]{2,1,0:T(8,128)S(1)}, f32[2,64,768]{2,1,0:T(8,128)S(1)}, f32[8,96,128]{2,1,0:T(8,128)S(1)}, f32[8,96,128]{2,1,0:T(8,128)S(1)}, f32[8,96,...) custom-call(s32[16]{0:T(128)} %bitcast.3, s32[16]{0:T(128)} %bitcast.4, s32[2]{0:T(128)} %bitcast.5, ...), custom_call_target="tpu_custom_call" | custom-call | tf_op jit(solution)/shard_map/step/pallas_call | solution.py:425
  44.2 1.5 %write_out.1 = (f32[2,64,512]{2,1,0:T(8,128)}, f32[2,64,768]{2,1,0:T(8,128)}, f32[8,96,128]{2,1,0:T(8,128)}, f32[8,96,128]{2,1,0:T(8,128)}, f32[8,96,128]{2,1,0:T(8,128)}, /*index=5*/f32[2,768,128]{2,1,0:T(8,128)}) custom-call(f32[2,64,512]{2,1,0:T(8,128)S(1)} %get-tuple-element.13.refs_0_, f32[2,64,768]{2,1,0:T(8,128)S(1)} %get-tuple-element.14.refs_1_, ...), custom_call_target="tpu_custom_call" | custom-call | tf_op jit(solution)/shard_map/write_out/pallas_call | solution.py:472

commit v5 on v4

--- a/solution.py
+++ b/solution.py
@@ -260,18 +260,23 @@
                 for c in range(chunks):
                     remote(grad_send.at[s, c, to], arrived.at[s, c, ep], es_sem.at[s, c], er_sem.at[s, c], to, dp).start()
 
-    rights = {}
+    seen, turned = set(), {}
     for b, (n, s, low, high) in enumerate(blocks):
         relay_block(*acts_kit(b))
         if b == 0:
             open_gate()
         finish_block(*acts_kit(b))
         left = split(acts_all[away[n], :, s, :, low:high].reshape(ndp * toks, high - low))
-        if s not in rights:
+        if s not in seen:
             for k in range(1, ndp):
                 grad_arrival(k, s).wait_recv()
-            rights[s] = split(g_cols[:, s].reshape(ndp * toks, cols))
-        grad = dot3(left, rights[s], ((0,), (0,)))
+            seen.add(s)
+        if b == 0:
+            grad = dot3(left, split(g_cols[:, s].reshape(ndp * toks, cols)), ((0,), (0,)))
+        else:
+            if s not in turned:
+                turned[s] = split(g_cols[:, s].reshape(ndp * toks, cols).T)
+            grad = dot3(turned[s], left, ((1,), (0,))).T
         base = away[n] * owners
         for i in range(owners):
             for c in range(chunks):

time: 45.9 us -> 45.7 us (level)
  no operation moved by 1% of the time
where the time goes in v5:
time: 45.7 us; the launch traced here: 45.4 us
  Pallas kernels  44.8 us (98%)
  between operations  0.64 us (1%)
    pallas_call x1, Pallas kernels, local_step(): pl.pallas_call(functools.partial(kernel, nep, ndp, slots), out_shape=shap...  43.3 us
    pallas_call x1, Pallas kernels, local_step(): pl.pallas_call(functools.partial(write_out, slots), out_shape=shapes, in_...  1.54 us

profile of v5, /device:TPU:0, one launch (start us, length us, event | category | flops | bytes accessed | tf_op | source)
XLA Modules:
  0.0 45.4 jit_solution(1166410736768107898)
XLA Ops:
  0.6 43.3 %step.1 = (f32[2,64,512]{2,1,0:T(8,128)S(1)}, f32[2,64,768]{2,1,0:T(8,128)S(1)}, f32[8,96,128]{2,1,0:T(8,128)S(1)}, f32[8,96,128]{2,1,0:T(8,128)S(1)}, f32[8,96,...) custom-call(s32[16]{0:T(128)} %bitcast.3, s32[16]{0:T(128)} %bitcast.4, s32[2]{0:T(128)} %bitcast.5, ...), custom_call_target="tpu_custom_call" | custom-call | tf_op jit(solution)/shard_map/step/pallas_call | solution.py:430
  43.9 1.5 %write_out.1 = (f32[2,64,512]{2,1,0:T(8,128)}, f32[2,64,768]{2,1,0:T(8,128)}, f32[8,96,128]{2,1,0:T(8,128)}, f32[8,96,128]{2,1,0:T(8,128)}, f32[8,96,128]{2,1,0:T(8,128)}, /*index=5*/f32[2,768,128]{2,1,0:T(8,128)}) custom-call(f32[2,64,512]{2,1,0:T(8,128)S(1)} %get-tuple-element.13.refs_0_, f32[2,64,768]{2,1,0:T(8,128)S(1)} %get-tuple-element.14.refs_1_, ...), custom_call_target="tpu_custom_call" | custom-call | tf_op jit(solution)/shard_map/write_out/pallas_call | solution.py:477

commit v6 on v5

--- a/solution.py
+++ b/solution.py
@@ -46,12 +46,11 @@
 
 
 def piece_blocks(sides, slots, width):
-    step = 128 if width % 128 == 0 else width
     found = []
     for s in range(slots):
         for n in range(sides):
-            size = step if n == 0 and s == 0 else width
-            found += [(n, s, low, low + size) for low in range(0, width, size)]
+            cuts = [0, 128, width] if n == 0 and s == 0 and width % 128 == 0 and width > 128 else [0, width]
+            found += [(n, s, low, high) for low, high in zip(cuts, cuts[1:])]
     return found
 
 

time: 45.7 us -> 46.5 us (1.018)
  Pallas kernels: 44.8 us -> 45.6 us
    pallas_call x1, Pallas kernels: 43.3 us -> 44.1 us  [local_step(): pl.pallas_call(functools.partial(kernel, nep, ndp, slots), out_shape=shap...]
where the time goes in v6:
time: 46.5 us; the launch traced here: 46.3 us
  Pallas kernels  45.6 us (98%)
  between operations  0.64 us (1%)
    pallas_call x1, Pallas kernels, local_step(): pl.pallas_call(functools.partial(kernel, nep, ndp, slots), out_shape=shap...  44.1 us
    pallas_call x1, Pallas kernels, local_step(): pl.pallas_call(functools.partial(write_out, slots), out_shape=shapes, in_...  1.54 us

profile of v6, /device:TPU:0, one launch (start us, length us, event | category | flops | bytes accessed | tf_op | source)
XLA Modules:
  0.0 46.3 jit_solution(905478810159039609)
XLA Ops:
  0.6 44.1 %step.1 = (f32[2,64,512]{2,1,0:T(8,128)S(1)}, f32[2,64,768]{2,1,0:T(8,128)S(1)}, f32[8,96,128]{2,1,0:T(8,128)S(1)}, f32[8,96,128]{2,1,0:T(8,128)S(1)}, f32[8,96,...) custom-call(s32[16]{0:T(128)} %bitcast.3, s32[16]{0:T(128)} %bitcast.4, s32[2]{0:T(128)} %bitcast.5, ...), custom_call_target="tpu_custom_call" | custom-call | tf_op jit(solution)/shard_map/step/pallas_call | solution.py:429
  44.7 1.5 %write_out.1 = (f32[2,64,512]{2,1,0:T(8,128)}, f32[2,64,768]{2,1,0:T(8,128)}, f32[8,96,128]{2,1,0:T(8,128)}, f32[8,96,128]{2,1,0:T(8,128)}, f32[8,96,128]{2,1,0:T(8,128)}, /*index=5*/f32[2,768,128]{2,1,0:T(8,128)}) custom-call(f32[2,64,512]{2,1,0:T(8,128)S(1)} %get-tuple-element.13.refs_0_, f32[2,64,768]{2,1,0:T(8,128)S(1)} %get-tuple-element.14.refs_1_, ...), custom_call_target="tpu_custom_call" | custom-call | tf_op jit(solution)/shard_map/write_out/pallas_call | solution.py:476
